TPU v7x, 32 devices: a whole 2x2x4 slice. The times are simulated.
32 devices in a mesh: row: 8 (over z, x), col: 4 (over y, core).
Axes of the slice: x: 2, y: 2, z: 4, core: 2. Of those that a mesh axis runs over, the one named last changes fastest.
Arguments:
- krylov_basis: float32 [4, 2, 3, 128, 128, 256], P(None, None, None, 'col', 'row'), may hold values from -50 to 50
- susceptibility: float32 [128, 128, 256], P('col', 'row'), may hold values from 0.1 to 1
- green_spectra: bfloat16 [6, 256, 256, 512], P(None, None, 'col', 'row'), may hold values from -3 to 3, as said below
Outputs:
- projections: float32 [4, 2, 2], replicated
- next_block: float32 [2, 3, 128, 128, 256], P(None, None, 'col', 'row')
- block_factor: float32 [2, 2], replicated
Inputs may be any that keep to these rules, and one draw needn't show every extreme that they name: `green_spectra`: each of the six arrays is even on the padded grid: its value at (a, b, c) equals its value at ((-a) mod 256, (-b) mod 256, (-c) mod 512).
All inputs are finite; a program needn't handle non-finite values.
Results may differ from a plain program's by a relative error of at most 0.0003.
Values sent between devices are 32-bit elements; how exact they have to be, the bound alone decides.
A program may use at most 192 MiB of HBM per device.

v0:
```python
import math

import jax
import jax.numpy as jnp
from jax import lax
from jax.sharding import PartitionSpec as P

GX = 256
GY = 128
GZ = 128
NB = 4


highest = lax.Precision.HIGHEST
tensor_pairs = ((0, 3, 4), (3, 1, 5), (4, 5, 2))


def twiddle(count_in, count_out, period, orient, factor):
    row_index = lax.broadcasted_iota(jnp.int32, (count_in, count_out), 0)
    col_index = lax.broadcasted_iota(jnp.int32, (count_in, count_out), 1)
    phases = row_index * col_index % period
    angles = phases.astype(jnp.float32) * (2.0 * math.pi / period)
    cosine = jnp.cos(angles) * factor
    sines = jnp.sin(angles) * (orient * factor)
    return jnp.stack([jnp.stack([cosine, sines]), jnp.stack([-sines, cosine])])


def exchange_rows(blocks):
    return lax.all_to_all(blocks, "row", split_axis=3, concat_axis=3, tiled=True)


def exchange_cols(blocks):
    return lax.all_to_all(blocks, "col", split_axis=3, concat_axis=3, tiled=True)


def convolve(source, green_spectra):
    row_count = lax.axis_size("row")
    col_count = lax.axis_size("col")
    width_x = 2 * GX
    width_y = 2 * GY
    width_z = 2 * GZ
    local_z = source.shape[-3]
    local_y = source.shape[-2]
    part_x = width_x // row_count
    part_y = width_y // col_count
    table_x = twiddle(GX, width_x, width_x, -1.0, 1.0).reshape(2, 2, GX, row_count, part_x)
    spectra = jnp.einsum("frczyx,rsxdl->fscdyzl", source, table_x, precision=highest)
    fields = spectra.shape[0]
    spectra = spectra.reshape(fields, 2, 3, row_count, local_y, local_z * part_x)
    spectra = exchange_rows(spectra)
    spectra = spectra.reshape(fields, 2, 3, GY, local_z, part_x)
    table_y = twiddle(GY, width_y, width_y, -1.0, 1.0).reshape(2, 2, GY, col_count, part_y)
    spectra = jnp.einsum("frcyzl,rsyeq->fscezql", spectra, table_y, precision=highest)
    spectra = spectra.reshape(fields, 2, 3, col_count, local_z, part_y * part_x)
    spectra = exchange_cols(spectra)
    spectra = spectra.reshape(fields, 2, 3, GZ, part_y * part_x)
    table_z = twiddle(GZ, width_z, width_z, -1.0, 1.0)
    spectra = jnp.einsum("frczb,rszk->fsckb", spectra, table_z, precision=highest)
    coupling = green_spectra.astype(jnp.float32).reshape(6, width_z, part_y * part_x)
    mixed = []
    for member in range(3):
        chosen = tensor_pairs[member]
        total = coupling[chosen[0]] * spectra[:, :, 0]
        total = total + coupling[chosen[1]] * spectra[:, :, 1]
        total = total + coupling[chosen[2]] * spectra[:, :, 2]
        mixed.append(total)
    spectra = jnp.stack(mixed, axis=2)
    back_z = twiddle(width_z, GZ, width_z, 1.0, 1.0)
    spectra = jnp.einsum("frckb,rskz->fsczb", spectra, back_z, precision=highest)
    spectra = spectra.reshape(fields, 2, 3, col_count, local_z, part_y * part_x)
    spectra = exchange_cols(spectra)
    spectra = spectra.reshape(fields, 2, 3, col_count, local_z, part_y, part_x)
    back_y = twiddle(width_y, GY, width_y, 1.0, 1.0).reshape(2, 2, col_count, part_y, GY)
    spectra = jnp.einsum("frcezql,rseqy->fscyzl", spectra, back_y, precision=highest)
    spectra = spectra.reshape(fields, 2, 3, row_count, local_y, local_z * part_x)
    spectra = exchange_rows(spectra)
    spectra = spectra.reshape(fields, 2, 3, row_count, local_y, local_z, part_x)
    scaling = 1.0 / (width_x * width_y * width_z)
    back_x = twiddle(width_x, GX, width_x, 1.0, scaling).reshape(2, 2, row_count, part_x, GX)
    result = jnp.einsum("frcdyzl,rsdlx->fsczyx", spectra, back_x, precision=highest)
    return result.reshape(2, 3, local_z, local_y, GX)


def per_device(krylov_basis, susceptibility, green_spectra):
    latest = krylov_basis[-1]
    response = convolve(latest[None], green_spectra)
    image = latest - susceptibility[None, None] * response
    entry_count = 3.0 * GX * GY * GZ
    flat_basis = krylov_basis.reshape(2 * NB, -1)
    flat_image = image.reshape(2, -1)
    local_coeffs = jnp.einsum("an,bn->ab", flat_basis, flat_image, precision=highest) / entry_count
    coefficients = lax.psum(local_coeffs, ("row", "col"))
    projected = flat_image - jnp.einsum("ab,an->bn", coefficients, flat_basis, precision=highest)
    local_gram = jnp.einsum("an,bn->ab", projected, projected, precision=highest) / entry_count
    gram = lax.psum(local_gram, ("row", "col"))
    lead_norm = jnp.sqrt(gram[0, 0] + 1e-06)
    cross_term = gram[0, 1] / lead_norm
    tail_norm = jnp.sqrt(gram[1, 1] - cross_term * cross_term + 1e-06)
    first_column = projected[0] / lead_norm
    second_column = (projected[1] - cross_term * first_column) / tail_norm
    next_block = jnp.stack([first_column, second_column]).reshape(image.shape)
    block_factor = jnp.stack(
        [jnp.stack([lead_norm, cross_term]), jnp.stack([jnp.zeros_like(lead_norm), tail_norm])]
    )
    return (coefficients.reshape(NB, 2, 2), next_block, block_factor)


def solution(mesh):
    in_specs = (
        P(None, None, None, "col", "row", None),
        P("col", "row", None),
        P(None, None, "col", "row"),
    )
    out_specs = (P(), P(None, None, "col", "row", None), P())
    return jax.shard_map(
        per_device, mesh=mesh, in_specs=in_specs, out_specs=out_specs, check_vma=False
    )
```

profile of v0, /device:TPU:0, one launch (start us, length us, event | category | flops | bytes accessed | tf_op | source)
XLA Modules:
  0.0 1139.6 jit_solution(13377161398254713833)
XLA Ops:
  7.2 23.1 %convolution_bitcast_fusion.1 = f32[1,2,3,8,16,32,64]{6,5,4,2,3,1,0:T(8,128)} fusion(f32[1,2,3,32,16,256]{5,4,3,2,1,0:T(8,128)S(1)} %slice.60, f32[1,1,256,8,64]{2,4,0,3,1:T(8,128)S(1)} %get-tuple-element.32, f32[1,1,256,8,64]{2,4,0,3,1:T(8,128)S(1)} %get-tuple-element.31, f32[1,1,256,8,64]{2,4,0,3,1:T(8,128)S(1)} %get-tuple-element.30), kind=kOutput, calls=%fused_computation.16 | convolution fusion | flops 9665249280 | bytes 11010048 | tf_op jit(solution)/shard_map/frczyx,rsxdl->fscdyzl/dot_general | solution.py:47
  30.3 11.7 %reshape.545 = f32[1,2,3,8,16,2048]{5,4,2,3,1,0:T(8,128)} reshape(f32[1,2,3,8,16,32,64]{6,5,4,2,3,1,0:T(8,128)} %convolution_bitcast_fusion.1) | data formatting | bytes 12582912 | tf_op jit(solution)/shard_map/reshape | solution.py:49
  56.4 137.5 %all-to-all-done = f32[1,2,3,8,16,2048]{5,4,2,1,0,3:T(8,128)} async-done(((f32[1,2,3,8,16,2048]{5,4,2,1,0,3:T(8,128)}), f32[1,2,3,8,16,2048]{5,4,2,1,0,3:T(8,128)}, u32[]{:S(2)}, u32[]{:S(2)}) %all-to-all-start) | async-done | bytes 6291488 | tf_op jit(solution)/shard_map/all_to_all | solution.py:29
  211.6 27.7 %fusion.9 = f32[1,2,3,4,32,64,64]{6,5,4,2,3,1,0:T(8,128)} fusion(f32[2,3,128,32,64,1,1]{4,3,2,1,0,6,5:T(8,128)} %bitcast.177, f32[1,1,128,4,64]{2,4,0,3,1:T(8,128)S(1)} %get-tuple-element.38, f32[1,1,128,4,64]{2,4,0,3,1:T(8,128)S(1)} %get-tuple-element.37, f32[1,1,128,4,64]{2,4,0,3,1:T(8,128)S(1)} %get-tuple-element.36), kind=kOutput, calls=%fused_computation.12 | convolution fusion | flops 9664069632 | bytes 19267584 | tf_op jit(solution)/shard_map/frcyzl,rsyeq->fscezql/dot_general | solution.py:53
  239.2 20.8 %reshape.547 = f32[1,2,3,4,32,4096]{5,4,2,3,1,0:T(8,128)} reshape(f32[1,2,3,4,32,64,64]{6,5,4,2,3,1,0:T(8,128)} %fusion.9) | data formatting | bytes 25165824 | tf_op jit(solution)/shard_map/reshape | solution.py:54
  277.4 11.8 %fusion.108 = (f32[1,256,64,64]{1,3,2,0:T(8,128)}, f32[1,256,64,64]{1,3,2,0:T(8,128)}, f32[1,256,64,64]{1,3,2,0:T(8,128)}, f32[1,256,64,64]{1,3,2,0:T(8,128)}, f...) fusion(bf16[6,256,64,64]{1,3,2,0:T(8,128)(2,1)} %param.5), kind=kLoop, calls=%fused_computation.152 | loop fusion | bytes 50331648 | tf_op jit(solution)/shard_map/slice | solution.py:63
  326.7 88.8 %all-to-all-done.1 = f32[1,2,3,4,32,4096]{5,4,2,1,0,3:T(8,128)} async-done(((f32[1,2,3,4,32,4096]{5,4,2,1,0,3:T(8,128)}), f32[1,2,3,4,32,4096]{5,4,2,1,0,3:T(8,128)}, u32[]{:S(2)}, u32[]{:S(2)}) %all-to-all-start.1) | async-done | bytes 12582944 | tf_op jit(solution)/shard_map/all_to_all | solution.py:33
  426.2 25.6 %convolution_bitcast_fusion = f32[1,2,3,256,4096]{4,3,2,1,0:T(8,128)} fusion(f32[2,3,128,4096,1]{3,2,0,1,4:T(8,128)} %bitcast.178, f32[1,2,128,256]{2,3,0,1:T(8,128)} %get-tuple-element.26, f32[1,2,128,256]{2,3,0,1:T(8,128)S(1)} %get-tuple-element.25), kind=kOutput, calls=%fused_computation.11 | convolution fusion | flops 19327483904 | bytes 38273024 | tf_op jit(solution)/shard_map/frczb,rszk->fsckb/dot_general | solution.py:58
  451.9 21.1 %multiply_add_fusion.2 = (f32[1,2,1,256,4096]{4,3,2,1,0:T(8,128)}, f32[1,2,1,256,4096]{4,3,2,1,0:T(8,128)}, f32[1,2,1,256,4096]{4,3,2,1,0:T(8,128)}) fusion(f32[1,2,3,256,4096]{4,3,2,1,0:T(8,128)} %convolution_bitcast_fusion, f32[256,4096]{1,0:T(8,128)S(1)} %copy-done.6, f32[256,4096]{1,0:T(8,128)S(1)} %copy-done.5, f32[256,4096]{1,0:T(8,128)S(1)} %copy-done.4, ...), kind=kLoop, calls=%fused_computation.15 | loop fusion | flops 31457280 | bytes 75497472 | tf_op jit(solution)/shard_map/add | solution.py:65
  473.0 26.6 %fusion.2 = f32[2,128,3,4096,1]{3,1,4,2,0:T(8,128)} fusion(f32[1,2,256,128]{2,3,0,1:T(8,128)} %get-tuple-element.24, f32[1,2,256,128]{2,3,0,1:T(8,128)S(1)} %copy-done.9, f32[1,2,1,256,4096]{4,3,2,1,0:T(8,128)} %get-tuple-element.16, f32[1,2,1,256,4096]{4,3,2,1,0:T(8,128)} %get-tuple-element.15, f32[1,2,1,256,4096]{4,3,2,1,0:T(8,128)} %get-tuple-element.14), kind=kOutput, calls=%fused_computation.4 | convolution fusion | flops 19340066816 | bytes 38273024 | tf_op jit(solution)/shard_map/frckb,rskz->fsczb/dot_general | solution.py:69
  517.2 137.5 %all-to-all-done.2 = f32[1,2,3,4,32,4096]{5,4,2,1,0,3:T(8,128)} async-done(((f32[1,2,3,4,32,4096]{5,4,2,1,0,3:T(8,128)}), f32[1,2,3,4,32,4096]{5,4,2,1,0,3:T(8,128)}, u32[]{:S(2)}, u32[]{:S(2)}) %all-to-all-start.2) | async-done | bytes 12582944 | tf_op jit(solution)/shard_map/all_to_all | solution.py:33
  654.7 20.5 %reshape.575 = f32[2,3,4,32,64,64]{5,4,3,1,0,2:T(8,128)} reshape(f32[1,2,3,4,32,4096]{5,4,2,1,0,3:T(8,128)} %all-to-all-done.2) | data formatting | bytes 25165824 | tf_op jit(solution)/shard_map/reshape.50
  675.2 46.1 %fusion.14 = f32[1,2,3,128,32,64]{3,5,4,2,1,0:T(8,128)} fusion(f32[2,3,4,32,64,64]{5,4,3,1,0,2:T(8,128)} %reshape.575, f32[1,1,4,64,128]{4,3,0,2,1:T(8,128)S(1)} %get-tuple-element.35, f32[1,1,4,64,128]{4,3,0,2,1:T(8,128)S(1)} %get-tuple-element.34, f32[1,1,4,64,128]{4,3,0,2,1:T(8,128)S(1)} %get-tuple-element.33), kind=kOutput, calls=%fused_computation.21 | convolution fusion | flops 9664069632 | bytes 19267584 | tf_op jit(solution)/shard_map/frcezql,rseqy->fscyzl/dot_general | solution.py:74
  721.3 12.7 %copy.62 = f32[1,2,3,128,32,64]{5,4,3,2,1,0:T(8,128)} copy(f32[1,2,3,128,32,64]{3,5,4,2,1,0:T(8,128)} %fusion.14) | data formatting | bytes 12582912 | tf_op jit(solution)/shard_map/frcezql,rseqy->fscyzl/transpose | solution.py:74
  734.0 11.7 %reshape.552 = f32[1,2,3,8,16,2048]{5,4,3,2,1,0:T(8,128)} reshape(f32[1,2,3,128,32,64]{5,4,3,2,1,0:T(8,128)} %copy.62) | data formatting | bytes 12582912 | tf_op jit(solution)/shard_map/reshape | solution.py:75
  777.4 117.4 %all-to-all-done.3 = f32[1,2,3,8,16,2048]{5,4,2,1,0,3:T(8,128)} async-done(((f32[1,2,3,8,16,2048]{5,4,2,1,0,3:T(8,128)}), f32[1,2,3,8,16,2048]{5,4,2,1,0,3:T(8,128)}, u32[]{:S(2)}, u32[]{:S(2)}) %all-to-all-start.3) | async-done | bytes 6291488 | tf_op jit(solution)/shard_map/all_to_all | solution.py:29
  905.2 12.7 %reshape.573 = f32[2,3,8,16,32,64,1]{5,4,0,2,3,1,6:T(8,128)} reshape(f32[1,2,3,8,16,2048]{5,1,3,4,2,0:T(2,128)} %copy.64) | data formatting | bytes 12582912 | tf_op jit(solution)/shard_map/reshape.52
  917.9 17.8 %multiply_subtract_fusion = (f32[1,2,3,32,16,256]{5,3,1,4,2,0:T(8,128)S(1)}, f32[1,2,3,32,16,256]{5,3,1,4,2,0:T(8,128)}) fusion(f32[1,2,3,32,16,256]{5,4,3,2,1,0:T(8,128)S(1)} %copy-done.1, f32[32,16,256]{2,0,1:T(8,128)} %copy.44, f32[2,3,8,16,32,64,1]{5,4,0,2,3,1,6:T(8,128)} %reshape.573, f32[1,1,8,64,256]{4,3,0,2,1:T(8,128)} %get-tuple-element.29, ...), kind=kOutput, calls=%fused_computation.19 | convolution fusion | flops 9666822144 | bytes 17825792 | tf_op jit(solution)/shard_map/frcdyzl,rsdlx->fsczyx/dot_general | solution.py:80
  943.1 29.7 %fusion.34 = f32[8,2]{0,1:T(2,128)S(1)} fusion(f32[2,393216]{1,0:T(2,128)S(1)} %sub.20, f32[8,393216]{1,0:T(8,128)} %reshape.554), kind=kOutput, calls=%fused_computation.42 | convolution fusion | flops 75497488 | bytes 15728704 | tf_op jit(solution)/shard_map/an,bn->ab/dot_general | solution.py:91
  974.9 37.7 %psum.14 = f32[8,2]{0,1:T(2,128)S(1)} all-reduce(f32[8,2]{0,1:T(2,128)S(1)} %fusion.34), channel_id=1, replica_groups=mesh['row'=8,'col'=4] {'row','col'}, use_global_device_ids=true, to_apply=%region_0.1 | all-reduce | flops 16 | bytes 128 | tf_op jit(solution)/shard_map/psum | solution.py:92
  1021.9 16.8 %convolution_subtract_fusion = f32[2,393216]{1,0:T(2,128)S(1)} fusion(f32[8,2]{0,1:T(2,128)S(1)} %psum.14, f32[8,393216]{1,0:T(8,128)} %reshape.554, f32[2,393216]{1,0:T(2,128)S(1)} %copy-done.2, f32[2,393216]{1,0:T(2,128)} %reshape.556, f32[393216]{0:T(1024)} %bitcast.186), kind=kOutput, calls=%fused_computation | convolution fusion | flops 77856768 | bytes 23593024 | tf_op jit(solution)/shard_map/ab,an->bn/dot_general | solution.py:93
  1040.4 28.0 %convolution_multiply_fusion.1 = f32[2,2]{1,0:T(2,128)S(1)} fusion(f32[2,393216]{1,0:T(2,128)S(1)} %convolution_subtract_fusion), kind=kOutput, calls=%fused_computation.43 | convolution fusion | flops 18874372 | bytes 3145744 | tf_op jit(solution)/shard_map/an,bn->ab/dot_general | solution.py:94
  1068.5 41.7 %psum.15 = f32[2,2]{1,0:T(2,128)S(1)} all-reduce(f32[2,2]{1,0:T(2,128)S(1)} %convolution_multiply_fusion.1), channel_id=1, replica_groups=mesh['row'=8,'col'=4] {'row','col'}, use_global_device_ids=true, to_apply=%region_1.2 | all-reduce | flops 4 | bytes 32 | tf_op jit(solution)/shard_map/psum | solution.py:95
  1112.9 21.1 %fusion.33 = (f32[393216]{0:T(1024)}, f32[1,393216]{1,0:T(1,128)S(1)}) fusion(f32[2,393216]{1,0:T(2,128)} %copy-done.3, f32[]{:T(128)} %sqrt.11, f32[]{:T(128)} %div.31, f32[]{:T(128)} %bitcast.62), kind=kLoop, calls=%fused_computation.40 | loop fusion | flops 1572864 | bytes 6291468 | tf_op jit(solution)/shard_map/div | solution.py:100
  (73 shorter events, 190.1 us)
Async XLA Ops:
  0.6 0.6 copy-start.10
  5.6 1.7 copy-start
  48.3 145.7 %all-to-all-start = ((f32[1,2,3,8,16,2048]{5,4,2,1,0,3:T(8,128)}), f32[1,2,3,8,16,2048]{5,4,2,1,0,3:T(8,128)}, u32[]{:S(2)}, u32[]{:S(2)}) async-start(f32[1,2,3,8,16,2048]{5,4,2,1,0,3:T(8,128)} %copy.48), calls=%async_computation | async-start | bytes 12582912 | tf_op jit(solution)/shard_map/all_to_all | solution.py:29
  270.7 144.8 %all-to-all-start.1 = ((f32[1,2,3,4,32,4096]{5,4,2,1,0,3:T(8,128)}), f32[1,2,3,4,32,4096]{5,4,2,1,0,3:T(8,128)}, u32[]{:S(2)}, u32[]{:S(2)}) async-start(f32[1,2,3,4,32,4096]{5,4,2,1,0,3:T(8,128)} %copy.51), calls=%async_computation.1 | async-start | bytes 25165824 | tf_op jit(solution)/shard_map/all_to_all | solution.py:33
  426.2 25.6 %copy-start.4 = (f32[256,4096]{1,0:T(8,128)S(1)}, f32[256,4096]{1,0:T(8,128)}, u32[]{:S(2)}) copy-start(f32[256,4096]{1,0:T(8,128)} %copy.46) | copy-start | bytes 12582916
  426.2 25.6 %copy-start.5 = (f32[256,4096]{1,0:T(8,128)S(1)}, f32[256,4096]{1,0:T(8,128)}, u32[]{:S(2)}) copy-start(f32[256,4096]{1,0:T(8,128)} %copy.53) | copy-start | bytes 12582916
  426.2 25.6 %copy-start.6 = (f32[256,4096]{1,0:T(8,128)S(1)}, f32[256,4096]{1,0:T(8,128)}, u32[]{:S(2)}) copy-start(f32[256,4096]{1,0:T(8,128)} %copy.54) | copy-start | bytes 12582916
  451.9 21.2 %copy-start.9 = (f32[1,2,256,128]{2,3,0,1:T(8,128)S(1)}, f32[1,2,256,128]{2,3,0,1:T(8,128)}, u32[]{:S(2)}) copy-start(f32[1,2,256,128]{2,3,0,1:T(8,128)} %get-tuple-element.23) | copy-start | bytes 786436
  510.3 144.5 %all-to-all-start.2 = ((f32[1,2,3,4,32,4096]{5,4,2,1,0,3:T(8,128)}), f32[1,2,3,4,32,4096]{5,4,2,1,0,3:T(8,128)}, u32[]{:S(2)}, u32[]{:S(2)}) async-start(f32[1,2,3,4,32,4096]{5,4,2,1,0,3:T(8,128)} %copy.59), calls=%async_computation.2 | async-start | bytes 25165824 | tf_op jit(solution)/shard_map/all_to_all | solution.py:33
  751.9 142.9 %all-to-all-start.3 = ((f32[1,2,3,8,16,2048]{5,4,2,1,0,3:T(8,128)}), f32[1,2,3,8,16,2048]{5,4,2,1,0,3:T(8,128)}, u32[]{:S(2)}, u32[]{:S(2)}) async-start(f32[1,2,3,8,16,2048]{5,4,2,1,0,3:T(8,128)} %copy.63), calls=%async_computation.3 | async-start | bytes 12582912 | tf_op jit(solution)/shard_map/all_to_all | solution.py:29
  756.7 11.5 %copy-start.1 = (f32[1,2,3,32,16,256]{5,4,3,2,1,0:T(8,128)S(1)}, f32[1,2,3,32,16,256]{5,4,3,2,1,0:T(8,128)}, u32[]{:S(2)}) copy-start(f32[1,2,3,32,16,256]{5,4,3,2,1,0:T(8,128)} %copy-done) | copy-start | bytes 9437188
  768.2 5.9 copy-start.11
  943.1 29.7 %copy-start.8 = (f32[32,16,256]{2,1,0:T(8,128)S(1)}, f32[32,16,256]{2,1,0:T(8,128)}, u32[]{:S(2)}) copy-start(f32[32,16,256]{2,1,0:T(8,128)} %param.4) | copy-start | bytes 1572868
  972.8 39.9 %copy-start.7 = (f32[1,2,3,32,16,256]{5,3,1,4,2,0:T(8,128)S(1)}, f32[1,2,3,32,16,256]{5,3,1,4,2,0:T(8,128)}, u32[]{:S(2)}) copy-start(f32[1,2,3,32,16,256]{5,3,1,4,2,0:T(8,128)} %get-tuple-element.43) | copy-start | bytes 9437188
  1016.1 5.8 copy-start.2
  1038.7 1.7 copy-start.3
where the time goes:
time: 1150 us; the launch traced here: 1140 us
  waiting for transfers between devices  481 us (42%)
  local copies, waits for them, and re-layouts  254 us (22%)
  matrix products  241 us (21%)
  blocking collectives  79.5 us (7%)
  other arithmetic  55.3 us (5%)
  starting transfers between devices  25.4 us (2%)
    all_to_all x2, waiting for transfers between devices, exchange_rows(): lax.all_to_all(blocks, 'row', split_axis=3, concat_axis=3, tiled=True)  255 us
    all_to_all x2, waiting for transfers between devices, exchange_cols(): lax.all_to_all(blocks, 'col', split_axis=3, concat_axis=3, tiled=True)  226 us
    dot_general x1, matrix products, convolve(): jnp.einsum('frcezql,rseqy->fscyzl', spectra, back_y, precision=highest)  46.1 us
    another operation x3, local copies, waits for them, and re-layouts  44.5 us
    reshape x3, local copies, waits for them, and re-layouts, convolve(): spectra = spectra.reshape(fields, 2, 3, col_count, local_z, part_y * part_x)  42.1 us
    psum x1, blocking collectives, per_device(): gram = lax.psum(local_gram, ('row', 'col'))  41.7 us
    psum x1, blocking collectives, per_device(): coefficients = lax.psum(local_coeffs, ('row', 'col'))  37.7 us
    reshape x4, local copies, waits for them, and re-layouts, convolve(): spectra.reshape(fields, 2, 3, row_count, local_y, local_z * part_x)  35.9 us
  transfers between devices with their start and end apart: 4, of which 4 were waited for; matrix products, arithmetic and copies ran while one was open for 6% of the time, Pallas kernels for 0%

commit v1 on v0

v1 whole, which is shorter than its diff:
```python
import math

import jax
import jax.numpy as jnp
from jax import lax
from jax.sharding import PartitionSpec as P

fast = lax.Precision.HIGH
tensor_pairs = ((0, 3, 4), (3, 1, 5), (4, 5, 2))


def twiddle(count_in, count_out, period, orient, factor):
    row_index = lax.broadcasted_iota(jnp.int32, (count_in, count_out), 0)
    col_index = lax.broadcasted_iota(jnp.int32, (count_in, count_out), 1)
    phases = row_index * col_index % period
    angles = phases.astype(jnp.float32) * (2.0 * math.pi / period)
    cosine = jnp.cos(angles) * factor
    sines = jnp.sin(angles) * (orient * factor)
    return jnp.stack([jnp.stack([cosine, sines]), jnp.stack([-sines, cosine])])


def exchange_rows(blocks):
    return lax.all_to_all(blocks, "row", split_axis=0, concat_axis=0, tiled=True)


def exchange_cols(blocks):
    return lax.all_to_all(blocks, "col", split_axis=0, concat_axis=0, tiled=True)


def forward(source, table_x, table_y, table_z):
    local_z, local_y = source.shape[1:3]
    row_count, part_x = table_x.shape[-2:]
    col_count, part_y = table_y.shape[-2:]
    spectra = jnp.einsum("rzyx,rsxdl->dsyzl", source, table_x, precision=fast)
    spectra = spectra.reshape(row_count, 2, local_y, local_z * part_x)
    spectra = exchange_rows(spectra)
    spectra = spectra.transpose(1, 0, 2, 3).reshape(2, row_count * local_y, local_z, part_x)
    spectra = jnp.einsum("ryzl,rsyeq->eszql", spectra, table_y, precision=fast)
    spectra = spectra.reshape(col_count, 2, local_z, part_y * part_x)
    spectra = exchange_cols(spectra)
    spectra = spectra.transpose(1, 0, 2, 3).reshape(2, col_count * local_z, part_y * part_x)
    return jnp.einsum("rzb,rszk->skb", spectra, table_z, precision=fast)


def backward(spectra, back_x, back_y, back_z):
    row_count, part_x = back_x.shape[2:4]
    col_count, part_y, width = back_y.shape[2:]
    spectra = jnp.einsum("rkb,rskz->szb", spectra, back_z, precision=fast)
    local_z = spectra.shape[1] // col_count
    spectra = spectra.reshape(2, col_count, local_z, part_y * part_x).transpose(1, 0, 2, 3)
    spectra = exchange_cols(spectra)
    spectra = spectra.reshape(col_count, 2, local_z, part_y, part_x)
    spectra = jnp.einsum("erzql,rseqy->syzl", spectra, back_y, precision=fast)
    local_y = width // row_count
    spectra = spectra.reshape(2, row_count, local_y, local_z * part_x).transpose(1, 0, 2, 3)
    spectra = exchange_rows(spectra)
    spectra = spectra.reshape(row_count, 2, local_y, local_z, part_x)
    return jnp.einsum("dryzl,rsdlx->szyx", spectra, back_x, precision=fast)


def convolve(source, green_spectra):
    row_count = lax.axis_size("row")
    col_count = lax.axis_size("col")
    width_x = 2 * source.shape[-1]
    width_y = 2 * source.shape[-2] * row_count
    width_z = 2 * source.shape[-3] * col_count
    part_x = width_x // row_count
    part_y = width_y // col_count
    half_x, half_y, half_z = width_x // 2, width_y // 2, width_z // 2
    table_x = twiddle(half_x, width_x, width_x, -1.0, 1.0).reshape(2, 2, half_x, row_count, part_x)
    table_y = twiddle(half_y, width_y, width_y, -1.0, 1.0).reshape(2, 2, half_y, col_count, part_y)
    table_z = twiddle(half_z, width_z, width_z, -1.0, 1.0)
    spectra = [forward(source[:, c], table_x, table_y, table_z) for c in range(3)]
    coupling = green_spectra.astype(jnp.float32).reshape(6, width_z, part_y * part_x)
    back_z = twiddle(width_z, half_z, width_z, 1.0, 1.0)
    back_y = twiddle(width_y, half_y, width_y, 1.0, 1.0).reshape(2, 2, col_count, part_y, half_y)
    scaling = 1.0 / (width_x * width_y * width_z)
    back_x = twiddle(width_x, half_x, width_x, 1.0, scaling).reshape(2, 2, row_count, part_x, half_x)
    result = []
    for member in range(3):
        chosen = tensor_pairs[member]
        total = coupling[chosen[0]] * spectra[0]
        total = total + coupling[chosen[1]] * spectra[1]
        total = total + coupling[chosen[2]] * spectra[2]
        result.append(backward(total, back_x, back_y, back_z))
    return result


def total_over_devices(partial):
    return jnp.sum(lax.all_gather(partial, ("row", "col")), axis=0)


def per_device(krylov_basis, susceptibility, green_spectra):
    blocks = krylov_basis.shape[0]
    latest = krylov_basis[-1]
    response = convolve(latest, green_spectra)
    image = [latest[:, c] - susceptibility[None] * response[c] for c in range(3)]
    image = jnp.stack(image, axis=1)
    entry_count = 3.0 * susceptibility.size * lax.axis_size("row") * lax.axis_size("col")
    basis = krylov_basis.reshape((2 * blocks,) + image.shape[1:])
    local_coeffs = jnp.stack(
        [jnp.sum(basis * image[j][None], axis=(1, 2, 3, 4)) for j in range(2)], axis=1
    )
    coefficients = total_over_devices(local_coeffs / entry_count)
    projected = []
    for j in range(2):
        column = image[j]
        for a in range(2 * blocks):
            column = column - coefficients[a, j] * basis[a]
        projected.append(column)
    g00 = jnp.sum(projected[0] * projected[0])
    g01 = jnp.sum(projected[0] * projected[1])
    g11 = jnp.sum(projected[1] * projected[1])
    gram = total_over_devices(jnp.stack([g00, g01, g11]) / entry_count)
    lead_norm = jnp.sqrt(gram[0] + 1e-06)
    cross_term = gram[1] / lead_norm
    tail_norm = jnp.sqrt(gram[2] - cross_term * cross_term + 1e-06)
    first_column = projected[0] / lead_norm
    second_column = (projected[1] - cross_term * first_column) / tail_norm
    next_block = jnp.stack([first_column, second_column])
    block_factor = jnp.stack(
        [jnp.stack([lead_norm, cross_term]), jnp.stack([jnp.zeros_like(lead_norm), tail_norm])]
    )
    return (coefficients.reshape(blocks, 2, 2), next_block, block_factor)


def solution(mesh):
    in_specs = (
        P(None, None, None, "col", "row", None),
        P("col", "row", None),
        P(None, None, "col", "row"),
    )
    out_specs = (P(), P(None, None, "col", "row", None), P())
    return jax.shard_map(
        per_device, mesh=mesh, in_specs=in_specs, out_specs=out_specs, check_vma=False
    )
```

time: 1150 us -> 842 us (0.73)
  waiting for transfers between devices: 481 us -> 219 us
  matrix products: 241 us -> 137 us
  starting transfers between devices: 25.4 us -> 59.5 us
  local copies, waits for them, and re-layouts: 254 us -> 287 us
    all_to_all x4 -> x12, waiting for transfers between devices: 481 us -> 219 us  [the longest x6 122 us: exchange_rows(): lax.all_to_all(blocks, 'row', split_axis=0, concat_axis=0, tiled=True)]
    dot_general x9 -> x18, matrix products: 241 us -> 137 us  [the longest x3 50.5 us: backward(): spectra = jnp.einsum('rkb,rskz->szb', spectra, back_z, precision=fast)]
    psum x2 -> x0, blocking collectives: 79.5 us -> none  [the longest x1 41.7 us: per_device(): gram = lax.psum(local_gram, ('row', 'col'))]
    all_gather x0 -> x2, blocking collectives: none -> 77.9 us  [total_over_devices(): return jnp.sum(lax.all_gather(partial, ('row', 'col')), axis=0)]
    reshape x10 -> x28, local copies, waits for them, and re-layouts: 95.3 us -> 155 us  [the longest x6 58 us: backward(): spectra = spectra.reshape(col_count, 2, local_z, part_y, part_x)]
    another operation x4 -> x2, local copies, waits for them, and re-layouts: 46.3 us -> 0.16 us  [per_device(): jnp.stack([jnp.sum(basis * image[j][None], axis=(1, 2, 3, 4)) for j in ra...]
    all_to_all x4 -> x12, starting transfers between devices: 25.4 us -> 59.5 us  [the longest x6 29.8 us: exchange_cols(): lax.all_to_all(blocks, 'col', split_axis=0, concat_axis=0, tiled=True)]
    dot_general x0 -> x6, local copies, waits for them, and re-layouts: none -> 28 us  [backward(): spectra = jnp.einsum('erzql,rseqy->syzl', spectra, back_y, precision=fast)]
  transfers between devices with their start and end apart: 4 -> 12, of which waited for: 4 -> 11; matrix products, arithmetic and copies ran while one was open for 6% -> 43% of each run, Pallas kernels for 0% -> 0%
where the time goes in v1:
time: 842 us; the launch traced here: 831 us
  local copies, waits for them, and re-layouts  287 us (34%)
  waiting for transfers between devices  219 us (26%)
  matrix products  137 us (16%)
  blocking collectives  77.9 us (9%)
  starting transfers between devices  59.5 us (7%)
  other arithmetic  47.7 us (6%)
    all_to_all x6, waiting for transfers between devices, exchange_rows(): lax.all_to_all(blocks, 'row', split_axis=0, concat_axis=0, tiled=True)  122 us
    all_to_all x6, waiting for transfers between devices, exchange_cols(): lax.all_to_all(blocks, 'col', split_axis=0, concat_axis=0, tiled=True)  96.4 us
    all_gather x2, blocking collectives, total_over_devices(): return jnp.sum(lax.all_gather(partial, ('row', 'col')), axis=0)  77.9 us
    reshape x6, local copies, waits for them, and re-layouts, backward(): spectra = spectra.reshape(col_count, 2, local_z, part_y, part_x)  58 us
    dot_general x3, matrix products, backward(): spectra = jnp.einsum('rkb,rskz->szb', spectra, back_z, precision=fast)  50.5 us
    reshape x6, local copies, waits for them, and re-layouts, forward(): spectra = spectra.reshape(col_count, 2, local_z, part_y * part_x)  37.7 us
    all_to_all x6, starting transfers between devices, exchange_cols(): lax.all_to_all(blocks, 'col', split_axis=0, concat_axis=0, tiled=True)  29.8 us
    all_to_all x6, starting transfers between devices, exchange_rows(): lax.all_to_all(blocks, 'row', split_axis=0, concat_axis=0, tiled=True)  29.6 us
  transfers between devices with their start and end apart: 12, of which 11 were waited for; matrix products, arithmetic and copies ran while one was open for 43% of the time, Pallas kernels for 0%

profile of v1, /device:TPU:0, one launch (start us, length us, event | category | flops | bytes accessed | tf_op | source)
XLA Modules:
  0.0 830.9 jit_solution(11497571219946661420)
XLA Ops:
  42.5 34.0 %all-to-all-done.2 = f32[8,2,16,2048]{3,2,1,0:T(8,128)} async-done(((f32[8,2,16,2048]{3,2,1,0:T(8,128)}), f32[8,2,16,2048]{3,2,1,0:T(8,128)}, u32[]{:S(2)}, u32[]{:S(2)}) %all-to-all-start.2) | async-done | bytes 2097184 | tf_op jit(solution)/shard_map/all_to_all | solution.py:23
  92.7 36.5 %all-to-all-done = f32[8,2,16,2048]{3,2,1,0:T(8,128)} async-done(((f32[8,2,16,2048]{3,2,1,0:T(8,128)}), f32[8,2,16,2048]{3,2,1,0:T(8,128)}, u32[]{:S(2)}, u32[]{:S(2)}) %all-to-all-start) | async-done | bytes 2097184 | tf_op jit(solution)/shard_map/all_to_all | solution.py:23
  139.0 8.8 %fusion.48 = f32[4,2,32,64,64]{4,3,2,0,1:T(8,128)} fusion(f32[2,128,32,64,1,1]{3,2,1,0,5,4:T(8,128)} %bitcast.624, f32[1,1,128,4,64]{2,4,0,3,1:T(8,128)S(1)} %get-tuple-element.39, f32[1,1,128,4,64]{2,4,0,3,1:T(8,128)S(1)} %get-tuple-element.38, f32[1,1,128,4,64]{2,4,0,3,1:T(8,128)S(1)} %get-tuple-element.37), kind=kOutput, calls=%fused_computation.57 | convolution fusion | flops 1611005952 | bytes 6684672 | tf_op jit(solution)/shard_map/ryzl,rsyeq->eszql/dot_general | solution.py:38
  160.3 21.0 %all-to-all-done.4 = f32[8,2,16,2048]{3,2,1,0:T(8,128)} async-done(((f32[8,2,16,2048]{3,2,1,0:T(8,128)}), f32[8,2,16,2048]{3,2,1,0:T(8,128)}, u32[]{:S(2)}, u32[]{:S(2)}) %all-to-all-start.4) | async-done | bytes 2097184 | tf_op jit(solution)/shard_map/all_to_all | solution.py:23
  212.5 22.1 %all-to-all-done.3 = f32[4,2,32,4096]{3,2,1,0:T(8,128)} async-done(((f32[4,2,32,4096]{3,2,1,0:T(8,128)}), f32[4,2,32,4096]{3,2,1,0:T(8,128)}, u32[]{:S(2)}, u32[]{:S(2)}) %all-to-all-start.3) | async-done | bytes 4194336 | tf_op jit(solution)/shard_map/all_to_all | solution.py:27
  244.2 8.8 %fusion.51 = f32[4,2,32,64,64]{4,3,2,0,1:T(8,128)} fusion(f32[2,128,32,64,1,1]{3,2,1,0,5,4:T(8,128)} %bitcast.620, f32[1,1,128,4,64]{2,4,0,3,1:T(8,128)S(1)} %get-tuple-element.39, f32[1,1,128,4,64]{2,4,0,3,1:T(8,128)S(1)} %get-tuple-element.38, f32[1,1,128,4,64]{2,4,0,3,1:T(8,128)S(1)} %get-tuple-element.37), kind=kOutput, calls=%fused_computation.58 | convolution fusion | flops 1611005952 | bytes 6684672 | tf_op jit(solution)/shard_map/ryzl,rsyeq->eszql/dot_general | solution.py:38
  265.7 21.9 %all-to-all-done.1 = f32[4,2,32,4096]{3,2,1,0:T(8,128)} async-done(((f32[4,2,32,4096]{3,2,1,0:T(8,128)}), f32[4,2,32,4096]{3,2,1,0:T(8,128)}, u32[]{:S(2)}, u32[]{:S(2)}) %all-to-all-start.1) | async-done | bytes 4194336 | tf_op jit(solution)/shard_map/all_to_all | solution.py:27
  292.7 11.7 %fusion.185 = (f32[1,256,64,64]{1,3,2,0:T(8,128)}, f32[1,256,64,64]{1,3,2,0:T(8,128)}, f32[1,256,64,64]{1,3,2,0:T(8,128)}, f32[1,256,64,64]{1,3,2,0:T(8,128)}, f...) fusion(bf16[6,256,64,64]{1,3,2,0:T(8,128)(2,1)} %param.5), kind=kLoop, calls=%fused_computation.253 | loop fusion | bytes 50331648 | tf_op jit(solution)/shard_map/slice | solution.py:82
  349.0 17.1 %fusion.4 = f32[2,128,4096,1]{2,1,3,0:T(8,128)} fusion(f32[2,256,4096,1]{2,1,3,0:T(8,128)} %fusion.128, f32[2,256,4096,1]{2,1,3,0:T(8,128)} %fusion.129, f32[2,256,4096,1]{2,1,3,0:T(8,128)} %fusion.130, f32[256,4096]{1,0:T(8,128)} %copy.98, f32[256,4096]{1,0:T(8,128)} %copy.92, f32[256,4096]{1,0:T(8,128)} %copy.85, ...), kind=kOutput, calls=%fused_computation.6 | convolution fusion | flops 3231842304 | bytes 42467328 | tf_op jit(solution)/shard_map/rkb,rskz->szb/dot_general | solution.py:48
  386.8 16.7 %fusion.2 = f32[2,128,4096,1]{2,1,3,0:T(8,128)} fusion(f32[2,256,4096,1]{2,1,3,0:T(8,128)} %fusion.128, f32[2,256,4096,1]{2,1,3,0:T(8,128)} %fusion.129, f32[2,256,4096,1]{2,1,3,0:T(8,128)} %fusion.130, f32[256,4096]{1,0:T(8,128)} %copy.109, f32[256,4096]{1,0:T(8,128)} %copy.108, f32[256,4096]{1,0:T(8,128)} %copy.92, ...), kind=kOutput, calls=%fused_computation.4 | convolution fusion | flops 3231842304 | bytes 42467328 | tf_op jit(solution)/shard_map/rkb,rskz->szb/dot_general | solution.py:48
  408.2 15.6 %all-to-all-done.6 = f32[4,2,32,4096]{3,2,1,0:T(8,128)} async-done(((f32[4,2,32,4096]{3,2,1,0:T(8,128)}), f32[4,2,32,4096]{3,2,1,0:T(8,128)}, u32[]{:S(2)}, u32[]{:S(2)}) %all-to-all-start.6) | async-done | bytes 4194336 | tf_op jit(solution)/shard_map/all_to_all | solution.py:27
  434.3 16.7 %fusion = f32[2,128,4096,1]{2,1,3,0:T(8,128)} fusion(f32[2,256,4096,1]{2,1,3,0:T(8,128)} %fusion.128, f32[2,256,4096,1]{2,1,3,0:T(8,128)} %fusion.129, f32[2,256,4096,1]{2,1,3,0:T(8,128)} %fusion.130, f32[256,4096]{1,0:T(8,128)} %copy.114, f32[256,4096]{1,0:T(8,128)} %copy.109, f32[256,4096]{1,0:T(8,128)} %copy.98, ...), kind=kOutput, calls=%fused_computation.2 | convolution fusion | flops 3231842304 | bytes 42467328 | tf_op jit(solution)/shard_map/rkb,rskz->szb/dot_general | solution.py:48
  455.7 21.2 %all-to-all-done.8 = f32[4,2,32,4096]{3,2,1,0:T(8,128)} async-done(((f32[4,2,32,4096]{3,2,1,0:T(8,128)}), f32[4,2,32,4096]{3,2,1,0:T(8,128)}, u32[]{:S(2)}, u32[]{:S(2)}) %all-to-all-start.8) | async-done | bytes 4194336 | tf_op jit(solution)/shard_map/all_to_all | solution.py:27
  491.1 11.4 %copy.205 = f32[4,2,32,64,64]{4,2,3,1,0:T(8,128)} copy(f32[4,2,32,64,64]{4,3,2,1,0:T(8,128)} %reshape.629) | data formatting | bytes 8388608 | tf_op jit(solution)/shard_map/reshape | solution.py:52
  515.8 14.4 %all-to-all-done.10 = f32[4,2,32,4096]{3,2,1,0:T(8,128)} async-done(((f32[4,2,32,4096]{3,2,1,0:T(8,128)}), f32[4,2,32,4096]{3,2,1,0:T(8,128)}, u32[]{:S(2)}, u32[]{:S(2)}) %all-to-all-start.10) | async-done | bytes 4194336 | tf_op jit(solution)/shard_map/all_to_all | solution.py:27
  542.0 11.4 %copy.204 = f32[4,2,32,64,64]{4,2,3,1,0:T(8,128)} copy(f32[4,2,32,64,64]{4,3,2,1,0:T(8,128)} %reshape.632) | data formatting | bytes 8388608 | tf_op jit(solution)/shard_map/reshape | solution.py:52
  566.6 15.5 %all-to-all-done.7 = f32[8,2,16,2048]{3,2,1,0:T(8,128)S(1)} async-done(((f32[8,2,16,2048]{3,2,1,0:T(8,128)}), f32[8,2,16,2048]{3,2,1,0:T(8,128)S(1)}, u32[]{:S(2)}, u32[]{:S(2)}) %all-to-all-start.7) | async-done | bytes 2097184 | tf_op jit(solution)/shard_map/all_to_all | solution.py:23
  594.9 11.4 %copy.203 = f32[4,2,32,64,64]{4,2,3,1,0:T(8,128)} copy(f32[4,2,32,64,64]{4,3,2,1,0:T(8,128)} %reshape.635) | data formatting | bytes 8388608 | tf_op jit(solution)/shard_map/reshape | solution.py:52
  619.5 15.2 %all-to-all-done.9 = f32[8,2,16,2048]{3,2,1,0:T(8,128)} async-done(((f32[8,2,16,2048]{3,2,1,0:T(8,128)}), f32[8,2,16,2048]{3,2,1,0:T(8,128)}, u32[]{:S(2)}, u32[]{:S(2)}) %all-to-all-start.9) | async-done | bytes 2097184 | tf_op jit(solution)/shard_map/all_to_all | solution.py:23
  639.3 20.0 %copy.122 = f32[4,2,3,32,16,256]{5,3,4,2,1,0:T(8,128)} copy(f32[4,2,3,32,16,256]{5,4,3,2,1,0:T(8,128)} %param.3) | data formatting | bytes 25165824 | tf_op args[0]
  710.1 41.2 %all_gather.8 = f32[32,8,2]{1,2,0:T(2,128)S(1)} all-gather(f32[1,8,2]{1,2,0:T(2,128)S(1)} %maximum_multiply_fusion), channel_id=1, replica_groups=mesh['row'=8,'col'=4] {'row','col'}, dimensions={0}, use_global_device_ids=true | all-gather | bytes 2112 | tf_op jit(solution)/shard_map/all_gather | solution.py:90
  752.2 16.3 %multiply_reduce_fusion.4 = (f32[]{:T(128)}, f32[]{:T(128)}, f32[]{:T(128)}) fusion(f32[8,3,32,16,256]{4,2,3,1,0:T(8,128)} %bitcast.598, f32[]{:T(128)} %bitcast.124, f32[]{:T(128)} %bitcast.122, f32[]{:T(128)} %bitcast.121, f32[]{:T(128)} %bitcast.120, f32[]{:T(128)} %bitcast.119, f32[]{:T(128)} %bitcast.118, f32[]{:T(128)} %bitcast.117, f32[]{:T(128)} %bitcast.115, ...), kind=kLoop, calls=%fused_computation.112 | loop fusion | flops 14942205 | bytes 15728716 | tf_op jit(solution)/shard_map/reduce_sum | solution.py:111
  770.3 36.7 %all-gather = f32[32,1,3]{2,1,0:T(1,128)S(1)} all-gather(f32[1,1,3]{2,1,0:T(1,128)S(1)} %fusion.168), channel_id=1, replica_groups=mesh['row'=8,'col'=4] {'row','col'}, dimensions={0}, use_global_device_ids=true | all-gather | bytes 396 | tf_op jit(solution)/shard_map/all_gather | solution.py:90
  809.6 15.7 %fusion.73 = (f32[1,3,32,16,256]{4,2,0,3,1:T(8,128)S(1)}, f32[1,3,32,16,256]{4,2,0,3,1:T(8,128)S(1)}) fusion(f32[2,3,32,16,256]{4,2,0,3,1:T(8,128)S(1)} %pad_maximum_fusion, f32[8,3,32,16,256]{4,2,3,1,0:T(8,128)} %bitcast.599, f32[]{:T(128)} %sqrt.11, f32[]{:T(128)} %div.28, f32[]{:T(128)} %bitcast.149, f32[]{:T(128)} %bitcast.147, f32[]{:T(128)} %bitcast.145, ...), kind=kLoop, calls=%fused_computation.85 | loop fusion | flops 14155776 | bytes 18874444 | tf_op jit(solution)/shard_map/div | solution.py:119
  (154 shorter events, 366.1 us)
Async XLA Ops:
  4.4 77.0 %copy-start = (f32[1,2,3,32,16,256]{5,3,1,4,2,0:T(8,128)}, f32[1,2,3,32,16,256]{5,3,1,4,2,0:T(8,128)S(1)}, u32[]{:S(2)}) copy-start(f32[1,2,3,32,16,256]{5,3,1,4,2,0:T(8,128)S(1)} %copy.209) | copy-start | bytes 9437188
  20.9 55.6 %all-to-all-start.2 = ((f32[8,2,16,2048]{3,2,1,0:T(8,128)}), f32[8,2,16,2048]{3,2,1,0:T(8,128)}, u32[]{:S(2)}, u32[]{:S(2)}) async-start(f32[8,2,16,2048]{3,2,1,0:T(8,128)} %copy.93), calls=%async_computation.2 | async-start | bytes 4194304 | tf_op jit(solution)/shard_map/all_to_all | solution.py:23
  76.5 52.6 %all-to-all-start = ((f32[8,2,16,2048]{3,2,1,0:T(8,128)}), f32[8,2,16,2048]{3,2,1,0:T(8,128)}, u32[]{:S(2)}, u32[]{:S(2)}) async-start(f32[8,2,16,2048]{3,2,1,0:T(8,128)} %copy.87), calls=%async_computation | async-start | bytes 4194304 | tf_op jit(solution)/shard_map/all_to_all | solution.py:23
  129.2 52.2 %all-to-all-start.4 = ((f32[8,2,16,2048]{3,2,1,0:T(8,128)}), f32[8,2,16,2048]{3,2,1,0:T(8,128)}, u32[]{:S(2)}, u32[]{:S(2)}) async-start(f32[8,2,16,2048]{3,2,1,0:T(8,128)} %copy.99), calls=%async_computation.4 | async-start | bytes 4194304 | tf_op jit(solution)/shard_map/all_to_all | solution.py:23
  181.3 53.2 %all-to-all-start.3 = ((f32[4,2,32,4096]{3,2,1,0:T(8,128)}), f32[4,2,32,4096]{3,2,1,0:T(8,128)}, u32[]{:S(2)}, u32[]{:S(2)}) async-start(f32[4,2,32,4096]{3,2,1,0:T(8,128)} %copy.96), calls=%async_computation.3 | async-start | bytes 8388608 | tf_op jit(solution)/shard_map/all_to_all | solution.py:27
  234.5 53.1 %all-to-all-start.1 = ((f32[4,2,32,4096]{3,2,1,0:T(8,128)}), f32[4,2,32,4096]{3,2,1,0:T(8,128)}, u32[]{:S(2)}, u32[]{:S(2)}) async-start(f32[4,2,32,4096]{3,2,1,0:T(8,128)} %copy.90), calls=%async_computation.1 | async-start | bytes 8388608 | tf_op jit(solution)/shard_map/all_to_all | solution.py:27
  287.6 53.3 %all-to-all-start.5 = ((f32[4,2,32,4096]{3,2,1,0:T(8,128)}), f32[4,2,32,4096]{3,2,1,0:T(8,128)}, u32[]{:S(2)}, u32[]{:S(2)}) async-start(f32[4,2,32,4096]{3,2,1,0:T(8,128)} %copy.102), calls=%async_computation.5 | async-start | bytes 8388608 | tf_op jit(solution)/shard_map/all_to_all | solution.py:27
  370.7 53.1 %all-to-all-start.6 = ((f32[4,2,32,4096]{3,2,1,0:T(8,128)}), f32[4,2,32,4096]{3,2,1,0:T(8,128)}, u32[]{:S(2)}, u32[]{:S(2)}) async-start(f32[4,2,32,4096]{3,2,1,0:T(8,128)} %bitcast.628), calls=%async_computation.6 | async-start | bytes 8388608 | tf_op jit(solution)/shard_map/all_to_all | solution.py:27
  423.8 53.1 %all-to-all-start.8 = ((f32[4,2,32,4096]{3,2,1,0:T(8,128)}), f32[4,2,32,4096]{3,2,1,0:T(8,128)}, u32[]{:S(2)}, u32[]{:S(2)}) async-start(f32[4,2,32,4096]{3,2,1,0:T(8,128)} %bitcast.627), calls=%async_computation.8 | async-start | bytes 8388608 | tf_op jit(solution)/shard_map/all_to_all | solution.py:27
  476.9 53.4 %all-to-all-start.10 = ((f32[4,2,32,4096]{3,2,1,0:T(8,128)}), f32[4,2,32,4096]{3,2,1,0:T(8,128)}, u32[]{:S(2)}, u32[]{:S(2)}) async-start(f32[4,2,32,4096]{3,2,1,0:T(8,128)} %bitcast.626), calls=%async_computation.10 | async-start | bytes 8388608 | tf_op jit(solution)/shard_map/all_to_all | solution.py:27
  530.2 51.9 %all-to-all-start.7 = ((f32[8,2,16,2048]{3,2,1,0:T(8,128)}), f32[8,2,16,2048]{3,2,1,0:T(8,128)S(1)}, u32[]{:S(2)}, u32[]{:S(2)}) async-start(f32[8,2,16,2048]{3,2,1,0:T(8,128)} %bitcast.633), calls=%async_computation.7 | async-start | bytes 4194304 | tf_op jit(solution)/shard_map/all_to_all | solution.py:23
  582.2 12.7 %copy-start.7 = (f32[8,2,16,2048]{3,2,1,0:T(8,128)}, f32[8,2,16,2048]{3,2,1,0:T(8,128)S(1)}, u32[]{:S(2)}) copy-start(f32[8,2,16,2048]{3,2,1,0:T(8,128)S(1)} %all-to-all-done.7) | copy-start | bytes 6291460
  582.2 52.6 %all-to-all-start.9 = ((f32[8,2,16,2048]{3,2,1,0:T(8,128)}), f32[8,2,16,2048]{3,2,1,0:T(8,128)}, u32[]{:S(2)}, u32[]{:S(2)}) async-start(f32[8,2,16,2048]{3,2,1,0:T(8,128)} %bitcast.632), calls=%async_computation.9 | async-start | bytes 4194304 | tf_op jit(solution)/shard_map/all_to_all | solution.py:23
  634.7 53.4 %all-to-all-start.11 = ((f32[8,2,16,2048]{3,2,1,0:T(8,128)}), f32[8,2,16,2048]{3,2,1,0:T(8,128)}, u32[]{:S(2)}, u32[]{:S(2)}) async-start(f32[8,2,16,2048]{3,2,1,0:T(8,128)} %bitcast.595), calls=%async_computation.11 | async-start | bytes 4194304 | tf_op jit(solution)/shard_map/all_to_all | solution.py:23
  639.3 20.0 %copy-start.14 = (f32[32,16,256]{2,1,0:T(8,128)S(1)}, f32[32,16,256]{2,1,0:T(8,128)}, u32[]{:S(2)}) copy-start(f32[32,16,256]{2,1,0:T(8,128)} %param.4) | copy-start | bytes 1572868
  639.3 21.1 %copy-start.16 = (s32[8,64]{1,0:T(8,128)S(1)}, s32[8,64]{1,0:T(8,128)}, u32[]{:S(2)}) copy-start(s32[8,64]{1,0:T(8,128)} %copy-done.15) | copy-start | bytes 6148
  673.9 5.5 copy-start.1
  679.4 5.9 copy-start.2
  679.4 5.9 copy-start.3
  679.4 5.9 copy-start.4
  679.4 5.9 copy-start.5
  679.4 5.9 copy-start.6
  698.0 5.4 copy-start.13
  698.0 7.9 slice-start
  (11 other events, 30.2 us)
